TPU v7x, 32 devices: a whole 2x2x4 slice. The times are simulated.
32 devices in a mesh: blk: 16 (over z, y, core), head: 2 (over x).
Axes of the slice: x: 2, y: 2, z: 4, core: 2. Of those that a mesh axis runs over, the one named last changes fastest.
Arguments:
- tokens: bfloat16 [2048, 3584], P(('blk', 'head')), may hold values from -100 to 100
- norm_gain: float32 [3584], replicated, may hold values from 0.1 to 1.9
- w_query: bfloat16 [3584, 3072], P('blk', 'head'), may hold values from -0.09375 to 0.09375
- w_key: bfloat16 [3584, 512], P('blk'), may hold values from -0.09375 to 0.09375
- w_value: bfloat16 [3584, 512], P('blk'), may hold values from -0.09375 to 0.09375
- q_bias: float32 [3072], P('head'), may hold values from -200 to 200
- k_bias: float32 [512], replicated, may hold values from -25 to 25
- v_bias: float32 [512], replicated, may hold values from -2.5 to 2.5
- w_out: bfloat16 [3072, 3584], P('head', 'blk'), may hold values from -0.109375 to 0.109375
Outputs:
- attention_out: bfloat16 [2048, 3584], P(('blk', 'head'))
All inputs are finite; a program needn't handle non-finite values.
Results may differ from a plain program's by a relative error of at most 0.04.
The roundings to bfloat16 on the way count: a program that leaves them out, or rounds other values in their place, can miss the bound.
Values may be sent and summed in bfloat16 or wider, within the bound.
A program may use at most 64 MiB of HBM per device.

v0:
```python
import math

import jax
import jax.numpy as jnp
from jax import lax
from jax.sharding import PartitionSpec as P

HD = 128
G = 6


theta_base = 1000000.0
eps_norm = 1e-06
masked_score = -1e30


def rotary_tables(positions, width):
    half = width // 2
    freq = theta_base ** (-(jnp.arange(half, dtype=jnp.float32) * 2.0 / width))
    angles = positions.astype(jnp.float32)[:, None] * freq[None, :]
    angles = jnp.concatenate([angles, angles], axis=1)
    return (jnp.cos(angles), jnp.sin(angles))


def rotate(values, cosine, sine):
    half = values.shape[-1] // 2
    turned = jnp.concatenate([-values[..., half:], values[..., :half]], axis=-1)
    return values * cosine[:, None, :] + turned * sine[:, None, :]


def block_width(rows, limit):
    width = min(rows, limit)
    while rows % width:
        width -= 1
    return width


def on_device(tokens, norm_gain, w_query, w_key, w_value, q_bias, k_bias, v_bias, w_out):
    head_count = lax.axis_size("head")
    head_index = lax.axis_index("head")
    block_index = lax.axis_index("blk")
    local_rows = tokens.shape[0]
    group_rows = local_rows * head_count
    heads_here = w_query.shape[1] // HD
    kv_here = max(1, heads_here // G)
    per_kv = heads_here // kv_here
    kv_first = head_index * heads_here // G
    scale = 1.0 / math.sqrt(HD)
    floats = tokens.astype(jnp.float32)
    normed = (
        floats * lax.rsqrt(jnp.mean(floats * floats, axis=1, keepdims=True) + eps_norm) * norm_gain
    ).astype(jnp.bfloat16)
    gathered = lax.all_gather(normed, "head", axis=0, tiled=True)
    key_cols = lax.dynamic_slice_in_dim(w_key, kv_first * HD, kv_here * HD, 1)
    value_cols = lax.dynamic_slice_in_dim(w_value, kv_first * HD, kv_here * HD, 1)
    pieces = (
        lax.all_gather(w_query, "blk", axis=0, tiled=True),
        lax.all_gather(key_cols, "blk", axis=0, tiled=True),
        lax.all_gather(value_cols, "blk", axis=0, tiled=True),
    )
    query_sum, key_sum, value_sum = tuple(
        (jnp.dot(gathered, piece, preferred_element_type=jnp.float32) for piece in pieces)
    )
    positions = block_index * group_rows + jnp.arange(group_rows, dtype=jnp.int32)
    cosine, sine = rotary_tables(positions, HD)
    key_bias_here = lax.dynamic_slice_in_dim(k_bias, kv_first * HD, kv_here * HD, 0)
    value_bias_here = lax.dynamic_slice_in_dim(v_bias, kv_first * HD, kv_here * HD, 0)
    query = rotate((query_sum + q_bias).reshape(group_rows, heads_here, HD), cosine, sine).astype(
        jnp.bfloat16
    )
    grouped = query.reshape(group_rows, kv_here, per_kv, HD)
    keys_here = rotate(
        (key_sum + key_bias_here).reshape(group_rows, kv_here, HD), cosine, sine
    ).astype(jnp.bfloat16)
    keys_here = keys_here.reshape(group_rows, kv_here * HD)
    values_here = (value_sum + value_bias_here).astype(jnp.bfloat16)
    last_query = block_index * group_rows + group_rows - 1
    initial = (
        jnp.full((kv_here, per_kv, group_rows), masked_score, jnp.float32),
        jnp.zeros((kv_here, per_kv, group_rows), jnp.float32),
        jnp.zeros((kv_here, per_kv, group_rows, HD), jnp.float32),
    )
    carry = initial
    pieces = (
        lax.all_gather(keys_here, "blk", axis=0, tiled=True),
        lax.all_gather(values_here, "blk", axis=0, tiled=True),
    )
    rows = pieces[0].shape[0]
    width = block_width(rows, 1024)
    count = rows // width
    key_stack = pieces[0].reshape(count, width, kv_here, HD)
    value_stack = pieces[1].reshape(count, width, kv_here, HD)
    offsets = jnp.arange(count, dtype=jnp.int32) * width

    def step(state, inputs):
        key_block, value_block, key_start = inputs

        def compute(current):
            top, total, acc = current
            scores = (
                jnp.einsum("rgqd,kgd->gqrk", grouped, key_block, preferred_element_type=jnp.float32)
                * scale
            )
            key_positions = key_start + jnp.arange(width, dtype=jnp.int32)
            visible = key_positions[None, :] <= positions[:, None]
            scores = jnp.where(visible, scores, masked_score)
            new_top = jnp.maximum(top, jnp.max(scores, axis=3))
            weights = jnp.where(visible, jnp.exp(scores - new_top[..., None]), 0.0)
            fade = jnp.exp(top - new_top)
            total = total * fade + jnp.sum(weights, axis=3)
            acc = acc * fade[..., None] + jnp.einsum(
                "gqrk,kgd->gqrd",
                weights.astype(jnp.bfloat16),
                value_block,
                preferred_element_type=jnp.float32,
            )
            return (new_top, total, acc)

        def keep(current):
            return current

        return (lax.cond(key_start <= last_query, compute, keep, state), None)

    carry, unused = lax.scan(step, carry, (key_stack, value_stack, offsets))
    top, total, acc = carry
    attended = (
        (acc / total[..., None])
        .transpose(2, 0, 1, 3)
        .reshape(group_rows, heads_here * HD)
        .astype(jnp.bfloat16)
    )
    out_cols = lax.all_gather(w_out, "blk", axis=1, tiled=True)
    return lax.psum_scatter(
        jnp.dot(attended, out_cols, preferred_element_type=jnp.float32).astype(jnp.bfloat16),
        "head",
        scatter_dimension=0,
        tiled=True,
    )


def solution(mesh):
    placed = (
        P(("blk", "head"), None),
        P(),
        P("blk", "head"),
        P("blk", None),
        P("blk", None),
        P("head"),
        P(),
        P(),
        P("head", "blk"),
    )
    return jax.shard_map(
        on_device, mesh=mesh, in_specs=placed, out_specs=P(("blk", "head"), None), check_vma=False
    )
```

profile of v0, /device:TPU:0, one launch (start us, length us, event | category | flops | bytes accessed | tf_op | source)
XLA Modules:
  0.0 388.7 jit_solution(11707920518854651433)
XLA Ops:
  6.5 0.9 copy-done
  7.5 0.7 constant_dynamic-slice_fusion.1
  8.2 1.6 constant_dynamic-slice_fusion
  9.8 0.8 dynamic_slice.34
  10.6 0.1 broadcast_multiply_fusion
  10.7 0.2 fusion.29
  10.9 0.1 copy.18
  11.0 0.1 copy.17
  11.1 1.2 fusion.22
  12.4 1.2 fusion.24
  13.6 14.2 %all_gather.21 = bf16[128,3584]{1,0:T(8,128)(2,1)S(1)} all-gather(bf16[64,3584]{1,0:T(8,128)(2,1)S(1)} %fusion.24), channel_id=1, replica_groups=mesh['blk'=16,'head'=2] {'head'}, dimensions={0}, use_global_device_ids=true | all-gather | bytes 1376256 | tf_op jit(solution)/shard_map/all_gather | solution.py:53
  27.7 25.3 %all-gather.7.cloned.1.call-done = bf16[3584,256]{1,0:T(8,128)(2,1)} async-done(((bf16[224,256]{1,0:T(8,128)(2,1)}), bf16[3584,256]{1,0:T(8,128)(2,1)}) %all-gather.7.cloned.1.call-update) | async-done | bytes 1835024 | tf_op jit(solution)/shard_map/all_gather | solution.py:58
  53.0 1.9 convolution_add_fusion.2
  55.0 0.2 slice_negate_fusion.1
  55.2 0.2 maximum_multiply_fusion.1
  55.5 0.7 fusion.27
  56.2 0.1 dynamic_slice.36
  56.3 38.5 %all-gather.13.cloned.1.call-done = bf16[3584,256]{1,0:T(8,128)(2,1)} async-done(((bf16[224,256]{1,0:T(8,128)(2,1)}), bf16[3584,256]{1,0:T(8,128)(2,1)}) %all-gather.13.cloned.1.call-update) | async-done | bytes 1835024 | tf_op jit(solution)/shard_map/all_gather | solution.py:59
  94.8 2.5 fusion.21
  97.4 0.5 all-gather.11.cloned.1.call-update
  98.0 0.5 all-gather.17.cloned.1.call-update
  98.6 0.2 reduce-scatter.2.cloned.1.call-start
  98.8 35.0 %all-gather.9.cloned.1.call-done = bf16[2048,256]{1,0:T(8,128)(2,1)} async-done(((bf16[128,256]{1,0:T(8,128)(2,1)}), bf16[2048,256]{1,0:T(8,128)(2,1)}) %all-gather.9.cloned.1.call-update) | async-done | bytes 1048592 | tf_op jit(solution)/shard_map/all_gather | solution.py:85
  133.8 1.3 reshape.107
  135.1 0.1 copy.21
  135.3 37.4 %all-gather.15.cloned.1.call-done = bf16[2048,256]{1,0:T(8,128)(2,1)} async-done(((bf16[128,256]{1,0:T(8,128)(2,1)}), bf16[2048,256]{1,0:T(8,128)(2,1)}) %all-gather.15.cloned.1.call-update) | async-done | bytes 1048592 | tf_op jit(solution)/shard_map/all_gather | solution.py:86
  172.6 1.3 reshape.110
  174.0 1.1 copy.23
  175.1 89.4 %all-gather.11.cloned.1.call-done = bf16[3584,1536]{1,0:T(8,128)(2,1)} async-done(((bf16[224,1536]{1,0:T(8,128)(2,1)}), bf16[3584,1536]{1,0:T(8,128)(2,1)}) %all-gather.11.cloned.1.call-update) | async-done | bytes 11010064 | tf_op jit(solution)/shard_map/all_gather | solution.py:57
  264.5 5.7 %convolution_add_fusion = f32[128,1536]{1,0:T(8,128)S(1)} fusion(bf16[128,3584]{1,0:T(8,128)(2,1)S(1)} %all_gather.21, bf16[3584,1536]{1,0:T(8,128)(2,1)} %all-gather.11.cloned.1.call-done, f32[1536]{0:T(1024)S(1)} %copy-done.2), kind=kOutput, calls=%fused_computation.25 | convolution fusion | flops 1409482752 | bytes 12720128 | tf_op jit(solution)/shard_map/dot_general | solution.py:62
  270.3 0.3 copy.19
  270.5 0.1 slice_negate_fusion
  270.6 0.1 fusion.26
  270.8 0.2 copy.22
  271.1 8.1 %while.15 = (s32[]{:T(128)}, f32[2,6,128]{2,1,0:T(8,128)S(1)}, f32[2,6,128]{2,1,0:T(8,128)S(1)}, f32[2,6,128,128]{3,2,1,0:T(8,128)S(1)}, s32[2]{0:T(128)S(1)}, /...) while((s32[]{:T(128)}, f32[2,6,128]{2,1,0:T(8,128)S(1)}, ...), condition=%wide.region_6.7_spmd.clone, body=%wide.region_1.6_spmd.clone.sunk | while | flops 826282112 | bytes 26720580 | solution.py:124
  271.1 0.6 dynamic_slice.51
  272.3 5.7 %conditional.3 = ((f32[2,6,128]{2,1,0:T(8,128)S(1)}, f32[2,6,128]{2,1,0:T(8,128)S(1)}, f32[2,6,128,128]{3,2,1,0:T(8,128)S(1)})) conditional(s32[]{:T(128)} %convert_element_type.75, (f32[2,6,128]{2,1,0:T(8,128)S(1)}, f32[2,6,128]{2,1,0:T(8,128)S(1)}, f32[2,6,128,128]{3,2,1,0:T(8,128)S(1)}) %tuple.43, (s32[]{:T(128)}, s32[]{:T(128)}, ...), branch_computations={%region_2.2_spmd, %region_3.5_spmd} | conditional | flops 826282112 | bytes 26719820 | solution.py:122
  272.3 0.6 iota_add_fusion
  272.9 0.2 broadcast_compare_fusion
  273.1 1.0 fusion.2
  274.1 1.5 fusion.4
  275.7 2.3 fusion.8
  278.0 0.6 dynamic_slice.51
  279.2 0.3 copy.24
  279.5 0.1 divide_convert_fusion
  279.6 76.1 %all-gather.17.cloned.1.call-done = bf16[1536,3584]{0,1:T(8,128)(2,1)} async-done(((bf16[1536,224]{0,1:T(8,128)(2,1)}), bf16[1536,3584]{0,1:T(8,128)(2,1)}) %all-gather.17.cloned.1.call-update) | async-done | bytes 11010064 | tf_op jit(solution)/shard_map/all_gather | solution.py:132
  355.7 8.7 %convolution_convert_fusion = bf16[128,3584]{1,0:T(8,128)(2,1)} fusion(bf16[128,1536]{0,1:T(8,128)(2,1)S(1)} %bitcast.58, bf16[1536,3584]{0,1:T(8,128)(2,1)} %all-gather.17.cloned.1.call-done), kind=kOutput, calls=%fused_computation.24 | convolution fusion | flops 1409744896 | bytes 12320768 | tf_op jit(solution)/shard_map/dot_general | solution.py:134
  364.5 17.3 %reduce-scatter.2.cloned.1.call-done = bf16[64,3584]{1,0:T(8,128)(2,1)} async-done(((bf16[128,3584]{1,0:T(8,128)(2,1)}), bf16[64,3584]{1,0:T(8,128)(2,1)}) %reduce-scatter.2.cloned.1.call-update) | async-done | bytes 458768 | tf_op jit(solution)/shard_map/reduce_scatter | solution.py:133
  (34 shorter events, 0.6 us)
Async XLA Ops:
  6.5 0.9 copy-start
  6.5 49.7 %copy-start.3 = (f32[512]{0:T(512)S(1)}, f32[512]{0:T(512)}, u32[]{:S(2)}) copy-start(f32[512]{0:T(512)} %param.20) | copy-start | bytes 6148
  6.5 46.5 %all-gather.7.cloned.1.call-start = ((), (), s32[]{:S(2)}) async-start(), calls=%async_computation.1 | async-start | bytes 1949696 | tf_op jit(solution)/shard_map/all_gather | solution.py:58
  8.2 86.7 %all-gather.13.cloned.1.call-start = ((), (), s32[]{:S(2)}) async-start(), calls=%async_computation.4 | async-start | bytes 1949696 | tf_op jit(solution)/shard_map/all_gather | solution.py:59
  9.8 124.0 %all-gather.9.cloned.1.call-start = ((), (), s32[]{:S(2)}) async-start(), calls=%async_computation.2 | async-start | bytes 1114112 | tf_op jit(solution)/shard_map/all_gather | solution.py:85
  56.2 116.5 %all-gather.15.cloned.1.call-start = ((), (), s32[]{:S(2)}) async-start(), calls=%async_computation.5 | async-start | bytes 1114112 | tf_op jit(solution)/shard_map/all_gather | solution.py:86
  56.3 208.2 %copy-start.2 = (f32[1536]{0:T(1024)S(1)}, f32[1536]{0:T(1024)}, u32[]{:S(2)}) copy-start(f32[1536]{0:T(1024)} %param.18) | copy-start | bytes 18436
  97.4 167.1 %all-gather.11.cloned.1.call-start = ((), (), s32[]{:S(2)}) async-start(), calls=%async_computation.3 | async-start | bytes 11698176 | tf_op jit(solution)/shard_map/all_gather | solution.py:57
  98.0 257.7 %all-gather.17.cloned.1.call-start = ((), (), s32[]{:S(2)}) async-start(), calls=%async_computation.6 | async-start | bytes 11698176 | tf_op jit(solution)/shard_map/all_gather | solution.py:132
  98.6 283.2 %reduce-scatter.2.cloned.1.call-start = ((), (), s32[]{:S(2)}) async-start(), calls=%async_computation.7 | async-start | bytes 1376256 | tf_op jit(solution)/shard_map/reduce_scatter | solution.py:133
  273.1 2.6 copy-start.1
Sparse Core Ops, SparseCore 0:
  9.6 43.3 all-gather.6
  55.3 39.4 all-gather.12
  97.0 36.7 all-gather.8
  135.8 36.8 all-gather.14
  174.8 89.7 all-gather.10
  266.7 88.9 all-gather.16
  364.6 17.1 reduce-scatter.1
where the time goes:
time: 389 us
  waiting for transfers between devices  320 us (82%)
  matrix products  22.2 us (6%)
  blocking collectives  14.2 us (4%)
  between operations  13.7 us (4%)
  local copies, waits for them, and re-layouts  10.2 us (3%)
  other arithmetic  6.38 us (2%)
    all_gather x1, waiting for transfers between devices, on_device(): lax.all_gather(w_query, 'blk', axis=0, tiled=True)  89.4 us
    all_gather x1, waiting for transfers between devices, on_device(): out_cols = lax.all_gather(w_out, 'blk', axis=1, tiled=True)  76.1 us
    all_gather x1, waiting for transfers between devices, on_device(): lax.all_gather(value_cols, 'blk', axis=0, tiled=True)  38.5 us
    all_gather x1, waiting for transfers between devices, on_device(): lax.all_gather(values_here, 'blk', axis=0, tiled=True)  37.4 us
    all_gather x1, waiting for transfers between devices, on_device(): lax.all_gather(keys_here, 'blk', axis=0, tiled=True)  35 us
    all_gather x1, waiting for transfers between devices, on_device(): lax.all_gather(key_cols, 'blk', axis=0, tiled=True)  25.3 us
    reduce_scatter x1, waiting for transfers between devices, on_device(): lax.psum_scatter(jnp.dot(attended, out_cols, preferred_element_type=jnp.f...  17.3 us
    all_gather x1, blocking collectives, on_device(): gathered = lax.all_gather(normed, 'head', axis=0, tiled=True)  14.2 us
  transfers between devices with their start and end apart: 7, of which 7 were waited for; matrix products, arithmetic and copies ran while one was open for 7% of the time, Pallas kernels for 0%

commit v1 on v0

v1 whole, which is shorter than its diff:
```python
import functools
import math

import jax
import jax.numpy as jnp
from jax import lax
from jax.experimental import pallas as pl
from jax.experimental.pallas import tpu as pltpu
from jax.sharding import PartitionSpec as P

HD = 128
G = 6
MESH = pl.DeviceIdType.MESH

theta_base = 1000000.0
eps_norm = 1e-06
masked_score = -1e30

WQ, WKV, WO, KV = range(4)
UP, DOWN, ACROSS, CORE = range(4)


def block_width(rows, limit):
    width = min(rows, limit)
    while rows % width:
        width -= 1
    return width


def kernel(
    sizes,
    tokens_ref,
    gain_ref,
    w_query_ref,
    w_key_ref,
    w_value_ref,
    q_bias_ref,
    k_bias_ref,
    v_bias_ref,
    w_out_ref,
    cos_ref,
    sin_ref,
    out_ref,
    wq,
    wkv,
    wo,
    kv,
    normed,
    query,
    attended,
    partial,
    outgoing,
    incoming,
    local_sem,
    send_sem,
    recv_sem,
    norm_send,
    norm_recv,
    sum_send,
    sum_recv,
):
    blocks, heads = sizes
    nz = blocks // 4
    me = lax.axis_index("blk")
    head = lax.axis_index("head")
    z, y, c = me // 4, (me // 2) % 2, me % 2
    local_rows, width = tokens_ref.shape
    group_rows = local_rows * heads
    heads_here = wq.shape[1] // HD
    kv_here = wkv.shape[1] // (2 * HD)
    per_kv = heads_here // kv_here
    kv_cols = kv_here * HD
    kv_start = pl.multiple_of((head * heads_here // G) * HD, HD)
    buffers = {WQ: wq, WKV: wkv, WO: wo, KV: kv}
    scale = 1.0 / math.sqrt(HD)

    def slot_of(zz, yy, cc):
        return (zz * 2 + yy) * 2 + cc

    def rows_of(item, slot):
        each = buffers[item].shape[0] // blocks
        return buffers[item].at[pl.ds(pl.multiple_of(slot * each, each), each)]

    def target(route):
        step = {UP: 4, DOWN: -4, ACROSS: 2 - 4 * y, CORE: 1 - 2 * c}[route]
        return (me + step, head)

    def copy(item, slot, route):
        part = rows_of(item, slot)
        return pltpu.make_async_remote_copy(
            src_ref=part,
            dst_ref=part,
            send_sem=send_sem.at[item, slot, route],
            recv_sem=recv_sem.at[item, slot],
            device_id=target(route),
            device_id_type=MESH,
        )

    def send(item, slot, route):
        if route == UP:
            pl.when(z < nz - 1)(lambda: copy(item, slot, route).start())
        elif route == DOWN:
            pl.when(z > 0)(lambda: copy(item, slot, route).start())
        else:
            copy(item, slot, route).start()

    def sent(item, slot, route):
        if route == UP:
            pl.when(z < nz - 1)(lambda: copy(item, slot, route).wait_send())
        elif route == DOWN:
            pl.when(z > 0)(lambda: copy(item, slot, route).wait_send())
        else:
            copy(item, slot, route).wait_send()

    def arrived(item, slot):
        copy(item, slot, CORE).wait_recv()

    def below(k, act):
        pl.when(z >= k)(lambda: act(z - k))

    def above(k, act):
        pl.when(z + k < nz)(lambda: act(z + k))

    def z_step(item, k, yy, then=()):
        def from_below(zz):
            slot = slot_of(zz, yy, c)
            arrived(item, slot)
            for route in (UP,) + then:
                send(item, slot, route)

        def from_above(zz):
            slot = slot_of(zz, yy, c)
            arrived(item, slot)
            for route in (DOWN,) + then:
                send(item, slot, route)

        below(k, from_below)
        above(k, from_above)

    def at_distance(k, act):
        if k == 0:
            act(z)
        else:
            below(k, act)
            above(k, act)

    def across(item, k):
        def act(zz):
            slot = slot_of(zz, 1 - y, c)
            arrived(item, slot)
            send(item, slot, CORE)

        at_distance(k, act)

    def finish(item):
        for zz in range(nz):
            for yy in range(2):
                arrived(item, slot_of(zz, yy, 1 - c))

    def drain(item, both):
        for yy in (y, 1 - y) if both else (y,):
            for route in (UP, DOWN):
                sent(item, slot_of(z, yy, c), route)
            for k in range(1, nz):
                below(k, lambda zz, yy=yy: sent(item, slot_of(zz, yy, c), UP))
                above(k, lambda zz, yy=yy: sent(item, slot_of(zz, yy, c), DOWN))
        if both:
            sent(item, me, ACROSS)
        for zz in range(nz):
            if not both:
                sent(item, slot_of(zz, y, c), ACROSS)
            for yy in range(2):
                sent(item, slot_of(zz, yy, c), CORE)

    own = [
        pltpu.make_async_copy(w_query_ref, rows_of(WQ, me), local_sem.at[0]),
        pltpu.make_async_copy(
            w_key_ref.at[:, pl.ds(kv_start, kv_cols)],
            rows_of(WKV, me).at[:, pl.ds(0, kv_cols)],
            local_sem.at[1],
        ),
        pltpu.make_async_copy(
            w_value_ref.at[:, pl.ds(kv_start, kv_cols)],
            rows_of(WKV, me).at[:, pl.ds(kv_cols, kv_cols)],
            local_sem.at[2],
        ),
        pltpu.make_async_copy(w_out_ref, rows_of(WO, me), local_sem.at[3]),
    ]
    for one in own:
        one.start()

    barrier = pltpu.get_barrier_semaphore()

    def greet(blk, hd):
        pl.semaphore_signal(barrier, inc=1, device_id=(blk, hd), device_id_type=MESH)

    pl.when(z < nz - 1)(lambda: greet(me + 4, head))
    pl.when(z > 0)(lambda: greet(me - 4, head))
    greet(target(ACROSS)[0], head)
    greet(target(CORE)[0], head)
    peers = [lax.rem(head + d, heads) for d in range(1, heads)]
    for peer in peers:
        greet(me, peer)
    ends = jnp.where(z < nz - 1, 1, 0) + jnp.where(z > 0, 1, 0)
    pl.semaphore_wait(barrier, ends + 2 + len(peers))

    for one in own:
        one.wait()
    for route in (UP, DOWN, ACROSS):
        send(WQ, me, route)
    for route in (ACROSS, UP, DOWN, CORE):
        send(WKV, me, route)
    send(WQ, me, CORE)

    my_rows = pl.ds(pl.multiple_of(head * local_rows, local_rows), local_rows)
    floats = tokens_ref[...].astype(jnp.float32)
    normed[my_rows, :] = (
        floats
        * lax.rsqrt(jnp.mean(floats * floats, axis=1, keepdims=True) + eps_norm)
        * gain_ref[...]
    ).astype(jnp.bfloat16)

    there = slot_of(z, 1 - y, c)
    arrived(WKV, there)
    for route in (UP, DOWN, CORE):
        send(WKV, there, route)

    def norm_copy(d):
        return pltpu.make_async_remote_copy(
            src_ref=normed.at[my_rows],
            dst_ref=normed.at[my_rows],
            send_sem=norm_send.at[d],
            recv_sem=norm_recv.at[d],
            device_id=(me, peers[d]),
            device_id_type=MESH,
        )

    for d in range(len(peers)):
        norm_copy(d).start()

    for k in range(1, nz):
        z_step(WQ, k, y, (ACROSS, CORE))
        z_step(WKV, k, y, (CORE,))
        z_step(WKV, k, 1 - y, (CORE,))
        if k == nz - 1:
            for route in (UP, DOWN):
                send(WO, me, route)
        across(WQ, k - 1)
    send(WO, me, ACROSS)
    send(WO, me, CORE)
    across(WQ, nz - 1)
    for d in range(len(peers)):
        norm_copy(d).wait_recv()
    z_step(WO, 1, y)
    finish(WQ)
    finish(WKV)

    cosine, sine = cos_ref[...], sin_ref[...]

    def turn(values):
        return values * cosine + pltpu.roll(values, HD // 2, 1) * sine

    kv_rows = pl.ds(pl.multiple_of(me * group_rows, group_rows), group_rows)
    sums = jnp.dot(normed[...], wkv[...], preferred_element_type=jnp.float32)
    for g in range(kv_here):
        bias = k_bias_ref[:, pl.ds(pl.multiple_of(kv_start + g * HD, HD), HD)]
        kv[kv_rows, pl.ds(g * HD, HD)] = turn(sums[:, g * HD : (g + 1) * HD] + bias).astype(
            jnp.bfloat16
        )
        bias = v_bias_ref[:, pl.ds(pl.multiple_of(kv_start + g * HD, HD), HD)]
        at = kv_cols + g * HD
        kv[kv_rows, pl.ds(at, HD)] = (sums[:, at : at + HD] + bias).astype(jnp.bfloat16)

    for route in (UP, DOWN, ACROSS, CORE):
        send(KV, me, route)

    joined = 2 if heads_here % 2 == 0 else 1

    def project(n, carry):
        cols = pl.ds(pl.multiple_of(n * joined * HD, joined * HD), joined * HD)
        total = jnp.dot(normed[...], wq[:, cols], preferred_element_type=jnp.float32)
        total = total + q_bias_ref[:, cols]
        for j in range(joined):
            query[n * joined + j] = turn(total[:, j * HD : (j + 1) * HD]).astype(jnp.bfloat16)
        return carry

    lax.fori_loop(0, heads_here // joined, project, 0)

    for k in range(1, nz):
        z_step(KV, k, y, (ACROSS, CORE))
        if k + 1 < nz:
            z_step(WO, k + 1, y)
    for k in range(nz):
        across(KV, k)
    for k in range(1, nz):
        at_distance(k, lambda zz: send(WO, slot_of(zz, y, c), ACROSS))
        at_distance(k, lambda zz: send(WO, slot_of(zz, y, c), CORE))
    finish(KV)

    keys = kv.shape[0]
    span = block_width(keys, 512)
    stacked = per_kv * group_rows
    last_query = me * group_rows + group_rows - 1
    steps = last_query // span + 1

    for g in range(kv_here):
        q = query[g * per_kv : (g + 1) * per_kv].reshape(stacked, HD)

        def attend(j, state, q=q, g=g):
            top, total, acc = state
            at = pl.ds(pl.multiple_of(j * span, span), span)
            scores = (
                lax.dot_general(
                    q,
                    kv[at, pl.ds(g * HD, HD)],
                    (((1,), (1,)), ((), ())),
                    preferred_element_type=jnp.float32,
                )
                * scale
            )
            shape = (per_kv, group_rows, span)
            rows = lax.broadcasted_iota(jnp.int32, shape, 1).reshape(stacked, span)
            columns = lax.broadcasted_iota(jnp.int32, (stacked, span), 1)
            visible = columns + j * span <= rows + me * group_rows
            scores = jnp.where(visible, scores, masked_score)
            new_top = jnp.maximum(top, jnp.max(scores, axis=1, keepdims=True))
            weights = jnp.where(visible, jnp.exp(scores - new_top), 0.0)
            fade = jnp.exp(top - new_top)
            total = total * fade + jnp.sum(weights, axis=1, keepdims=True)
            acc = acc * fade + jnp.dot(
                weights.astype(jnp.bfloat16),
                kv[at, pl.ds(kv_cols + g * HD, HD)],
                preferred_element_type=jnp.float32,
            )
            return (new_top, total, acc)

        start = (
            jnp.full((stacked, 1), masked_score, jnp.float32),
            jnp.zeros((stacked, 1), jnp.float32),
            jnp.zeros((stacked, HD), jnp.float32),
        )
        top, total, acc = lax.fori_loop(0, steps, attend, start)
        result = (acc / total).astype(jnp.bfloat16)
        for r in range(per_kv):
            attended[:, pl.ds((g * per_kv + r) * HD, HD)] = result[
                r * group_rows : (r + 1) * group_rows
            ]

    for k in range(nz):
        across(WO, k)
    finish(WO)

    chunk = 256

    def produce(n, carry):
        cols = pl.ds(pl.multiple_of(n * chunk, chunk), chunk)
        result = lax.dot_general(
            attended[...],
            wo[cols, :],
            (((1,), (1,)), ((), ())),
            preferred_element_type=jnp.float32,
        )
        partial[:, cols] = result
        outgoing[:, cols] = result.astype(jnp.bfloat16)
        return carry

    lax.fori_loop(0, width // chunk, produce, 0)

    def sum_copy(d):
        rows = pl.ds(pl.multiple_of(peers[d] * local_rows, local_rows), local_rows)
        return pltpu.make_async_remote_copy(
            src_ref=outgoing.at[rows],
            dst_ref=incoming.at[d],
            send_sem=sum_send.at[d],
            recv_sem=sum_recv.at[d],
            device_id=(me, peers[d]),
            device_id_type=MESH,
        )

    for d in range(len(peers)):
        sum_copy(d).start()
    for item in (WQ, WKV, WO, KV):
        drain(item, item == WKV)
    for d in range(len(peers)):
        norm_copy(d).wait_send()
    for d in range(len(peers)):
        sum_copy(d).wait_recv()
    result = partial[my_rows, :]
    for d in range(len(peers)):
        result = result + incoming[d].astype(jnp.float32)
    out_ref[...] = result.astype(jnp.bfloat16)
    for d in range(len(peers)):
        sum_copy(d).wait_send()


def on_device(tokens, norm_gain, w_query, w_key, w_value, q_bias, k_bias, v_bias, w_out):
    blocks, heads = lax.axis_size("blk"), lax.axis_size("head")
    local_rows, width = tokens.shape
    group_rows = local_rows * heads
    heads_here = w_query.shape[1] // HD
    kv_here = max(1, heads_here // G)
    positions = lax.axis_index("blk") * group_rows + jnp.arange(group_rows, dtype=jnp.int32)
    half = HD // 2
    freq = theta_base ** (-(jnp.arange(half, dtype=jnp.float32) * 2.0 / HD))
    angles = positions.astype(jnp.float32)[:, None] * freq[None, :]
    cosine, sine = jnp.cos(angles), jnp.sin(angles)
    cosine = jnp.concatenate([cosine, cosine], axis=1)
    sine = jnp.concatenate([-sine, sine], axis=1)
    inner = heads_here * HD
    vmem = pl.BlockSpec(memory_space=pltpu.VMEM)
    hbm = pl.BlockSpec(memory_space=pl.ANY)
    others = max(1, heads - 1)
    bf16, f32 = jnp.bfloat16, jnp.float32
    return pl.pallas_call(
        functools.partial(kernel, (blocks, heads)),
        out_shape=jax.ShapeDtypeStruct((local_rows, width), bf16),
        in_specs=[vmem, vmem, hbm, hbm, hbm, vmem, vmem, vmem, hbm, vmem, vmem],
        out_specs=vmem,
        scratch_shapes=[
            pltpu.VMEM((width, inner), bf16),
            pltpu.VMEM((width, 2 * kv_here * HD), bf16),
            pltpu.VMEM((width, inner), bf16),
            pltpu.VMEM((blocks * group_rows, 2 * kv_here * HD), bf16),
            pltpu.VMEM((group_rows, width), bf16),
            pltpu.VMEM((heads_here, group_rows, HD), bf16),
            pltpu.VMEM((group_rows, inner), bf16),
            pltpu.VMEM((group_rows, width), f32),
            pltpu.VMEM((group_rows, width), bf16),
            pltpu.VMEM((others, local_rows, width), bf16),
            pltpu.SemaphoreType.DMA((4,)),
            pltpu.SemaphoreType.DMA((4, blocks, 4)),
            pltpu.SemaphoreType.DMA((4, blocks)),
            pltpu.SemaphoreType.DMA((others,)),
            pltpu.SemaphoreType.DMA((others,)),
            pltpu.SemaphoreType.DMA((others,)),
            pltpu.SemaphoreType.DMA((others,)),
        ],
        compiler_params=pltpu.CompilerParams(
            collective_id=0, has_side_effects=True, vmem_limit_bytes=60 * 1024 * 1024
        ),
    )(
        tokens,
        norm_gain[None, :],
        w_query,
        w_key,
        w_value,
        q_bias[None, :],
        k_bias[None, :],
        v_bias[None, :],
        w_out.T,
        cosine,
        sine,
    )


def solution(mesh):
    placed = (
        P(("blk", "head"), None),
        P(),
        P("blk", "head"),
        P("blk", None),
        P("blk", None),
        P("head"),
        P(),
        P(),
        P("head", "blk"),
    )
    return jax.shard_map(
        on_device, mesh=mesh, in_specs=placed, out_specs=P(("blk", "head"), None), check_vma=False
    )
```

time: 389 us -> 208 us (0.53)
  waiting for transfers between devices: 320 us -> 0 us
  Pallas kernels: 0 us -> 202 us
  matrix products: 22.2 us -> 0 us
  blocking collectives: 14.2 us -> 0 us
  between operations: 13.7 us -> 0.02 us
  local copies, waits for them, and re-layouts: 10.2 us -> 3.7 us
  other arithmetic: 6.38 us -> 1.07 us
    all_gather x6 -> x0, waiting for transfers between devices: 302 us -> none  [the longest x1 89.4 us: on_device(): lax.all_gather(w_query, 'blk', axis=0, tiled=True)]
    pallas_call x0 -> x1, Pallas kernels: none -> 202 us  [on_device(): pl.pallas_call(functools.partial(kernel, (blocks, heads)), out_shape=jax....]
    dot_general x6 -> x0, matrix products: 22.2 us -> none  [the longest x3 10.2 us: on_device(): jnp.dot(gathered, piece, preferred_element_type=jnp.float32)]
    reduce_scatter x1 -> x0, waiting for transfers between devices: 17.3 us -> none  [on_device(): lax.psum_scatter(jnp.dot(attended, out_cols, preferred_element_type=jnp.f...]
    all_gather x1 -> x0, blocking collectives: 14.2 us -> none  [on_device(): gathered = lax.all_gather(normed, 'head', axis=0, tiled=True)]
    dynamic_slice x6 -> x0, local copies, waits for them, and re-layouts: 4.21 us -> none  [the longest x1 1.56 us: on_device(): lax.dynamic_slice_in_dim(w_value, kv_first * HD, kv_here * HD, 1)]
  transfers between devices with their start and end apart: 7 -> 0, of which waited for: 7 -> 0; matrix products, arithmetic and copies ran while one was open for 7% -> 0% of each run, Pallas kernels for 0% -> 0%
where the time goes in v1:
time: 208 us; the launch traced here: 207 us
  Pallas kernels  202 us (97%)
  local copies, waits for them, and re-layouts  3.7 us (2%)
    pallas_call x1, Pallas kernels, on_device(): pl.pallas_call(functools.partial(kernel, (blocks, heads)), out_shape=jax....  202 us

profile of v1, /device:TPU:0, one launch (start us, length us, event | category | flops | bytes accessed | tf_op | source)
XLA Modules:
  0.0 207.1 jit_solution(2729206459741004584)
XLA Ops:
  0.0 0.0 copy-start.1
  0.0 0.0 copy-start
  0.0 0.7 copy-done.1
  0.7 0.6 broadcast_in_dim.15.q_bias_ref
  1.3 0.0 copy-done
  1.3 0.6 broadcast_in_dim.14.gain_ref
  1.9 0.3 fusion
  2.2 0.7 pad_maximum_fusion
  3.0 202.3 %shard_map.91 = bf16[64,3584]{1,0:T(8,128)(2,1)} custom-call(bf16[64,3584]{1,0:T(8,128)(2,1)} %tokens_ref.1, f32[1,3584]{1,0:T(1,128)} %broadcast_in_dim.14.gain_ref, bf16[224,1536]{1,0:T(8,128)(2,1)} %w_query_ref.1, bf16[224,512]{1,0:T(8,128)(2,1)} %w_key_ref.1, bf16[224,512]{1,0:T(8,128)(2,1)} %w_value_ref.1, f32[1,1536]{1,0:T(1,128)} %broadcast_in_dim.15.q_bias_ref, ...), custom_call_target="tpu_custom_call" | custom-call | tf_op jit(solution)/shard_map/pallas_call | solution.py:414
  205.3 1.8 copy.11
  (2 shorter events, 0.0 us)
Async XLA Ops:
  0.0 0.7 copy-start.1
  0.0 1.3 copy-start

commit v2 on v1

--- a/solution.py
+++ b/solution.py
@@ -204,13 +204,16 @@
     ends = jnp.where(z < nz - 1, 1, 0) + jnp.where(z > 0, 1, 0)
     pl.semaphore_wait(barrier, ends + 2 + len(peers))
 
-    for one in own:
-        one.wait()
-    for route in (UP, DOWN, ACROSS):
-        send(WQ, me, route)
+    own[1].wait()
+    own[2].wait()
     for route in (ACROSS, UP, DOWN, CORE):
         send(WKV, me, route)
-    send(WQ, me, CORE)
+    own[0].wait()
+    own[3].wait()
+    for route in (ACROSS, CORE):
+        send(WQ, me, route)
+    for route in (ACROSS, CORE):
+        send(WO, me, route)
 
     my_rows = pl.ds(pl.multiple_of(head * local_rows, local_rows), local_rows)
     floats = tokens_ref[...].astype(jnp.float32)
@@ -239,20 +242,16 @@
         norm_copy(d).start()
 
     for k in range(1, nz):
-        z_step(WQ, k, y, (ACROSS, CORE))
         z_step(WKV, k, y, (CORE,))
         z_step(WKV, k, 1 - y, (CORE,))
-        if k == nz - 1:
+        if k == max(1, nz - 2):
             for route in (UP, DOWN):
-                send(WO, me, route)
-        across(WQ, k - 1)
-    send(WO, me, ACROSS)
-    send(WO, me, CORE)
-    across(WQ, nz - 1)
+                send(WQ, me, route)
+    if nz == 1:
+        for route in (UP, DOWN):
+            send(WQ, me, route)
     for d in range(len(peers)):
         norm_copy(d).wait_recv()
-    z_step(WO, 1, y)
-    finish(WQ)
     finish(WKV)
 
     cosine, sine = cos_ref[...], sin_ref[...]
@@ -271,8 +270,27 @@
         at = kv_cols + g * HD
         kv[kv_rows, pl.ds(at, HD)] = (sums[:, at : at + HD] + bias).astype(jnp.bfloat16)
 
+    across(WQ, 0)
     for route in (UP, DOWN, ACROSS, CORE):
         send(KV, me, route)
+
+    for k in range(1, nz):
+        z_step(WQ, k, y, (ACROSS, CORE))
+        if k == max(1, nz - 2):
+            for route in (UP, DOWN):
+                send(WO, me, route)
+        z_step(KV, k, y, (ACROSS, CORE))
+    if nz == 1:
+        for route in (UP, DOWN):
+            send(WO, me, route)
+    for k in range(1, nz):
+        if k == nz - 1:
+            z_step(WO, 1, y, (ACROSS, CORE))
+        across(WQ, k)
+    for k in range(nz):
+        across(KV, k)
+    finish(WQ)
+    finish(KV)
 
     joined = 2 if heads_here % 2 == 0 else 1
 
@@ -285,17 +303,6 @@
         return carry
 
     lax.fori_loop(0, heads_here // joined, project, 0)
-
-    for k in range(1, nz):
-        z_step(KV, k, y, (ACROSS, CORE))
-        if k + 1 < nz:
-            z_step(WO, k + 1, y)
-    for k in range(nz):
-        across(KV, k)
-    for k in range(1, nz):
-        at_distance(k, lambda zz: send(WO, slot_of(zz, y, c), ACROSS))
-        at_distance(k, lambda zz: send(WO, slot_of(zz, y, c), CORE))
-    finish(KV)
 
     keys = kv.shape[0]
     span = block_width(keys, 512)
@@ -345,15 +352,31 @@
             attended[:, pl.ds((g * per_kv + r) * HD, HD)] = result[
                 r * group_rows : (r + 1) * group_rows
             ]
-
-    for k in range(nz):
-        across(WO, k)
-    finish(WO)
-
-    chunk = 256
-
-    def produce(n, carry):
-        cols = pl.ds(pl.multiple_of(n * chunk, chunk), chunk)
+        if 2 + g < nz:
+            z_step(WO, 2 + g, y, (ACROSS, CORE))
+
+    for k in range(2 + kv_here, nz):
+        z_step(WO, k, y, (ACROSS, CORE))
+
+    each = wo.shape[0] // blocks
+    grouped = (4 * each) % HD == 0
+    groups = nz if grouped else 1
+    chunk = width // groups
+
+    def sum_copy(d, i, start):
+        rows = pl.ds(pl.multiple_of(peers[d] * local_rows, local_rows), local_rows)
+        cols = pl.ds(pl.multiple_of(start, HD), chunk)
+        return pltpu.make_async_remote_copy(
+            src_ref=outgoing.at[rows, cols],
+            dst_ref=incoming.at[d, :, cols],
+            send_sem=sum_send.at[d, i],
+            recv_sem=sum_recv.at[d, i],
+            device_id=(me, peers[d]),
+            device_id_type=MESH,
+        )
+
+    def produce(start, size):
+        cols = pl.ds(pl.multiple_of(start, HD), size)
         result = lax.dot_general(
             attended[...],
             wo[cols, :],
@@ -362,35 +385,54 @@
         )
         partial[:, cols] = result
         outgoing[:, cols] = result.astype(jnp.bfloat16)
-        return carry
-
-    lax.fori_loop(0, width // chunk, produce, 0)
-
-    def sum_copy(d):
-        rows = pl.ds(pl.multiple_of(peers[d] * local_rows, local_rows), local_rows)
-        return pltpu.make_async_remote_copy(
-            src_ref=outgoing.at[rows],
-            dst_ref=incoming.at[d],
-            send_sem=sum_send.at[d],
-            recv_sem=sum_recv.at[d],
-            device_id=(me, peers[d]),
-            device_id_type=MESH,
-        )
-
-    for d in range(len(peers)):
-        sum_copy(d).start()
+
+    def place(i):
+        way = 1 - 2 * (z // max(1, nz // 2)) if nz > 1 else 1
+        return lax.rem(z + way * i + nz, nz)
+
+    if grouped:
+
+        def produce_group(i, carry):
+            zz = place(i)
+            slot = slot_of(zz, 1 - y, c)
+            arrived(WO, slot)
+            send(WO, slot, CORE)
+            for yy in range(2):
+                arrived(WO, slot_of(zz, yy, 1 - c))
+            produce(zz * 4 * each, chunk)
+            for d in range(len(peers)):
+                sum_copy(d, i, zz * chunk).start()
+            return carry
+
+        lax.fori_loop(0, nz, produce_group, 0)
+    else:
+        for k in range(nz):
+            across(WO, k)
+        finish(WO)
+        part = 256
+        lax.fori_loop(0, width // part, lambda n, carry: (produce(n * part, part), carry)[1], 0)
+        for d in range(len(peers)):
+            sum_copy(d, 0, 0).start()
+
     for item in (WQ, WKV, WO, KV):
         drain(item, item == WKV)
     for d in range(len(peers)):
         norm_copy(d).wait_send()
-    for d in range(len(peers)):
-        sum_copy(d).wait_recv()
-    result = partial[my_rows, :]
-    for d in range(len(peers)):
-        result = result + incoming[d].astype(jnp.float32)
-    out_ref[...] = result.astype(jnp.bfloat16)
-    for d in range(len(peers)):
-        sum_copy(d).wait_send()
+
+    def collect(i, carry):
+        start = place(i) * chunk if grouped else 0
+        cols = pl.ds(pl.multiple_of(start, HD), chunk)
+        for d in range(len(peers)):
+            sum_copy(d, i, start).wait_recv()
+        result = partial[my_rows, cols]
+        for d in range(len(peers)):
+            result = result + incoming[d, :, cols].astype(jnp.float32)
+        out_ref[:, cols] = result.astype(jnp.bfloat16)
+        for d in range(len(peers)):
+            sum_copy(d, i, start).wait_send()
+        return carry
+
+    lax.fori_loop(0, groups, collect, 0)
 
 
 def on_device(tokens, norm_gain, w_query, w_key, w_value, q_bias, k_bias, v_bias, w_out):
@@ -432,8 +474,8 @@
             pltpu.SemaphoreType.DMA((4, blocks)),
             pltpu.SemaphoreType.DMA((others,)),
             pltpu.SemaphoreType.DMA((others,)),
-            pltpu.SemaphoreType.DMA((others,)),
-            pltpu.SemaphoreType.DMA((others,)),
+            pltpu.SemaphoreType.DMA((others, blocks // 4)),
+            pltpu.SemaphoreType.DMA((others, blocks // 4)),
         ],
         compiler_params=pltpu.CompilerParams(
             collective_id=0, has_side_effects=True, vmem_limit_bytes=60 * 1024 * 1024

time: 208 us -> 166 us (0.80)
  Pallas kernels: 202 us -> 159 us
    pallas_call x1, Pallas kernels: 202 us -> 159 us  [on_device(): pl.pallas_call(functools.partial(kernel, (blocks, heads)), out_shape=jax....]
where the time goes in v2:
time: 166 us; the launch traced here: 164 us
  Pallas kernels  159 us (96%)
  local copies, waits for them, and re-layouts  3.7 us (2%)
    pallas_call x1, Pallas kernels, on_device(): pl.pallas_call(functools.partial(kernel, (blocks, heads)), out_shape=jax....  159 us

profile of v2, /device:TPU:0, one launch (start us, length us, event | category | flops | bytes accessed | tf_op | source)
XLA Modules:
  0.0 163.9 jit_solution(10845651921540193150)
XLA Ops:
  0.0 0.0 copy-start.1
  0.0 0.0 copy-start
  0.0 0.7 copy-done.1
  0.7 0.6 broadcast_in_dim.15.q_bias_ref
  1.3 0.0 copy-done
  1.3 0.6 broadcast_in_dim.14.gain_ref
  1.9 0.3 fusion
  2.2 0.7 pad_maximum_fusion
  3.0 159.1 %shard_map.91 = bf16[64,3584]{1,0:T(8,128)(2,1)} custom-call(bf16[64,3584]{1,0:T(8,128)(2,1)} %tokens_ref.1, f32[1,3584]{1,0:T(1,128)} %broadcast_in_dim.14.gain_ref, bf16[224,1536]{1,0:T(8,128)(2,1)} %w_query_ref.1, bf16[224,512]{1,0:T(8,128)(2,1)} %w_key_ref.1, bf16[224,512]{1,0:T(8,128)(2,1)} %w_value_ref.1, f32[1,1536]{1,0:T(1,128)} %broadcast_in_dim.15.q_bias_ref, ...), custom_call_target="tpu_custom_call" | custom-call | tf_op jit(solution)/shard_map/pallas_call | solution.py:456
  162.1 1.8 %copy.11 = bf16[64,3584]{1,0:T(8,128)(2,1)} copy(bf16[64,3584]{1,0:T(8,128)(2,1)} %shard_map.91) | data formatting | bytes 917504
  (2 shorter events, 0.0 us)
Async XLA Ops:
  0.0 0.7 copy-start.1
  0.0 1.3 copy-start

commit v3 on v2

--- a/solution.py
+++ b/solution.py
@@ -16,7 +16,7 @@
 eps_norm = 1e-06
 masked_score = -1e30
 
-WQ, WKV, WO, KV = range(4)
+WQ, WKV, WO, KV, WQ_TAIL, WO_TAIL = range(6)
 UP, DOWN, ACROSS, CORE = range(4)
 
 
@@ -71,7 +71,8 @@
     per_kv = heads_here // kv_here
     kv_cols = kv_here * HD
     kv_start = pl.multiple_of((head * heads_here // G) * HD, HD)
-    buffers = {WQ: wq, WKV: wkv, WO: wo, KV: kv}
+    buffers = {WQ: wq, WKV: wkv, WO: wo, KV: kv, WQ_TAIL: wq, WO_TAIL: wo}
+    queries, outs = (WQ, WQ_TAIL), (WO, WO_TAIL)
     scale = 1.0 / math.sqrt(HD)
 
     def slot_of(zz, yy, cc):
@@ -79,7 +80,15 @@
 
     def rows_of(item, slot):
         each = buffers[item].shape[0] // blocks
-        return buffers[item].at[pl.ds(pl.multiple_of(slot * each, each), each)]
+        first, size = 0, each
+        if item in queries + outs:
+            cut = each // 2 // 16 * 16
+            first, size = (0, cut) if item in (WQ, WO) else (cut, each - cut)
+        return buffers[item].at[pl.ds(pl.multiple_of(slot * each + first, 16), size)]
+
+    def whole_rows(ref):
+        each = ref.shape[0] // blocks
+        return ref.at[pl.ds(pl.multiple_of(me * each, each), each)]
 
     def target(route):
         step = {UP: 4, DOWN: -4, ACROSS: 2 - 4 * y, CORE: 1 - 2 * c}[route]
@@ -173,7 +182,7 @@
                 sent(item, slot_of(zz, yy, c), CORE)
 
     own = [
-        pltpu.make_async_copy(w_query_ref, rows_of(WQ, me), local_sem.at[0]),
+        pltpu.make_async_copy(w_query_ref, whole_rows(wq), local_sem.at[0]),
         pltpu.make_async_copy(
             w_key_ref.at[:, pl.ds(kv_start, kv_cols)],
             rows_of(WKV, me).at[:, pl.ds(0, kv_cols)],
@@ -184,7 +193,7 @@
             rows_of(WKV, me).at[:, pl.ds(kv_cols, kv_cols)],
             local_sem.at[2],
         ),
-        pltpu.make_async_copy(w_out_ref, rows_of(WO, me), local_sem.at[3]),
+        pltpu.make_async_copy(w_out_ref, whole_rows(wo), local_sem.at[3]),
     ]
     for one in own:
         one.start()
@@ -210,10 +219,9 @@
         send(WKV, me, route)
     own[0].wait()
     own[3].wait()
-    for route in (ACROSS, CORE):
-        send(WQ, me, route)
-    for route in (ACROSS, CORE):
-        send(WO, me, route)
+    for item in queries + outs:
+        for route in (ACROSS, CORE):
+            send(item, me, route)
 
     my_rows = pl.ds(pl.multiple_of(head * local_rows, local_rows), local_rows)
     floats = tokens_ref[...].astype(jnp.float32)
@@ -245,11 +253,9 @@
         z_step(WKV, k, y, (CORE,))
         z_step(WKV, k, 1 - y, (CORE,))
         if k == max(1, nz - 2):
-            for route in (UP, DOWN):
-                send(WQ, me, route)
-    if nz == 1:
-        for route in (UP, DOWN):
-            send(WQ, me, route)
+            for item in queries:
+                for route in (UP, DOWN):
+                    send(item, me, route)
     for d in range(len(peers)):
         norm_copy(d).wait_recv()
     finish(WKV)
@@ -270,27 +276,29 @@
         at = kv_cols + g * HD
         kv[kv_rows, pl.ds(at, HD)] = (sums[:, at : at + HD] + bias).astype(jnp.bfloat16)
 
-    across(WQ, 0)
+    for item in queries:
+        across(item, 0)
     for route in (UP, DOWN, ACROSS, CORE):
         send(KV, me, route)
 
     for k in range(1, nz):
-        z_step(WQ, k, y, (ACROSS, CORE))
+        for item in queries:
+            z_step(item, k, y, (ACROSS, CORE))
+        z_step(KV, k, y, (ACROSS, CORE))
         if k == max(1, nz - 2):
-            for route in (UP, DOWN):
-                send(WO, me, route)
-        z_step(KV, k, y, (ACROSS, CORE))
-    if nz == 1:
-        for route in (UP, DOWN):
-            send(WO, me, route)
+            for item in outs:
+                for route in (UP, DOWN):
+                    send(item, me, route)
     for k in range(1, nz):
         if k == nz - 1:
-            z_step(WO, 1, y, (ACROSS, CORE))
-        across(WQ, k)
+            for item in outs:
+                z_step(item, 1, y, (ACROSS, CORE))
+        for item in queries:
+            across(item, k)
     for k in range(nz):
         across(KV, k)
-    finish(WQ)
-    finish(KV)
+    for item in queries + (KV,):
+        finish(item)
 
     joined = 2 if heads_here % 2 == 0 else 1
 
@@ -303,6 +311,10 @@
         return carry
 
     lax.fori_loop(0, heads_here // joined, project, 0)
+
+    if nz > 2:
+        for item in outs:
+            z_step(item, 2, y, (ACROSS, CORE))
 
     keys = kv.shape[0]
     span = block_width(keys, 512)
@@ -352,11 +364,11 @@
             attended[:, pl.ds((g * per_kv + r) * HD, HD)] = result[
                 r * group_rows : (r + 1) * group_rows
             ]
-        if 2 + g < nz:
-            z_step(WO, 2 + g, y, (ACROSS, CORE))
-
-    for k in range(2 + kv_here, nz):
-        z_step(WO, k, y, (ACROSS, CORE))
+        for k in range(3, nz):
+            if g == 0:
+                z_step(WO, k, y, (ACROSS, CORE))
+    for k in range(3, nz):
+        z_step(WO_TAIL, k, y, (ACROSS, CORE))
 
     each = wo.shape[0] // blocks
     grouped = (4 * each) % HD == 0
@@ -395,10 +407,12 @@
         def produce_group(i, carry):
             zz = place(i)
             slot = slot_of(zz, 1 - y, c)
-            arrived(WO, slot)
-            send(WO, slot, CORE)
-            for yy in range(2):
-                arrived(WO, slot_of(zz, yy, 1 - c))
+            for item in outs:
+                arrived(item, slot)
+                send(item, slot, CORE)
+            for item in outs:
+                for yy in range(2):
+                    arrived(item, slot_of(zz, yy, 1 - c))
             produce(zz * 4 * each, chunk)
             for d in range(len(peers)):
                 sum_copy(d, i, zz * chunk).start()
@@ -406,15 +420,16 @@
 
         lax.fori_loop(0, nz, produce_group, 0)
     else:
-        for k in range(nz):
-            across(WO, k)
-        finish(WO)
+        for item in outs:
+            for k in range(nz):
+                across(item, k)
+            finish(item)
         part = 256
         lax.fori_loop(0, width // part, lambda n, carry: (produce(n * part, part), carry)[1], 0)
         for d in range(len(peers)):
             sum_copy(d, 0, 0).start()
 
-    for item in (WQ, WKV, WO, KV):
+    for item in queries + outs + (WKV, KV):
         drain(item, item == WKV)
     for d in range(len(peers)):
         norm_copy(d).wait_send()
@@ -470,8 +485,8 @@
             pltpu.VMEM((group_rows, width), bf16),
             pltpu.VMEM((others, local_rows, width), bf16),
             pltpu.SemaphoreType.DMA((4,)),
-            pltpu.SemaphoreType.DMA((4, blocks, 4)),
-            pltpu.SemaphoreType.DMA((4, blocks)),
+            pltpu.SemaphoreType.DMA((6, blocks, 4)),
+            pltpu.SemaphoreType.DMA((6, blocks)),
             pltpu.SemaphoreType.DMA((others,)),
             pltpu.SemaphoreType.DMA((others,)),
             pltpu.SemaphoreType.DMA((others, blocks // 4)),

time: 166 us -> 161 us (0.970); the launches traced: 164 us -> 161 us
  Pallas kernels: 159 us -> 156 us
    pallas_call x1, Pallas kernels: 159 us -> 156 us  [on_device(): pl.pallas_call(functools.partial(kernel, (blocks, heads)), out_shape=jax....]
where the time goes in v3:
time: 161 us
  Pallas kernels  156 us (97%)
  local copies, waits for them, and re-layouts  3.7 us (2%)
    pallas_call x1, Pallas kernels, on_device(): pl.pallas_call(functools.partial(kernel, (blocks, heads)), out_shape=jax....  156 us

profile of v3, /device:TPU:0, one launch (start us, length us, event | category | flops | bytes accessed | tf_op | source)
XLA Modules:
  0.0 161.0 jit_solution(15214871503936972167)
XLA Ops:
  0.0 0.0 copy-start.1
  0.0 0.0 copy-start
  0.0 0.7 copy-done.1
  0.7 0.6 broadcast_in_dim.15.q_bias_ref
  1.3 0.0 copy-done
  1.3 0.6 broadcast_in_dim.14.gain_ref
  1.9 0.3 fusion
  2.2 0.7 pad_maximum_fusion
  3.0 156.2 %shard_map.91 = bf16[64,3584]{1,0:T(8,128)(2,1)} custom-call(bf16[64,3584]{1,0:T(8,128)(2,1)} %tokens_ref.1, f32[1,3584]{1,0:T(1,128)} %broadcast_in_dim.14.gain_ref, bf16[224,1536]{1,0:T(8,128)(2,1)} %w_query_ref.1, bf16[224,512]{1,0:T(8,128)(2,1)} %w_key_ref.1, bf16[224,512]{1,0:T(8,128)(2,1)} %w_value_ref.1, f32[1,1536]{1,0:T(1,128)} %broadcast_in_dim.15.q_bias_ref, ...), custom_call_target="tpu_custom_call" | custom-call | tf_op jit(solution)/shard_map/pallas_call | solution.py:471
  159.2 1.8 %copy.11 = bf16[64,3584]{1,0:T(8,128)(2,1)} copy(bf16[64,3584]{1,0:T(8,128)(2,1)} %shard_map.91) | data formatting | bytes 917504
  (2 shorter events, 0.0 us)
Async XLA Ops:
  0.0 0.7 copy-start.1
  0.0 1.3 copy-start

commit v4 on v3

--- a/solution.py
+++ b/solution.py
@@ -16,7 +16,7 @@
 eps_norm = 1e-06
 masked_score = -1e30
 
-WQ, WKV, WO, KV, WQ_TAIL, WO_TAIL = range(6)
+WQ, WKV, WO, KV, WQ_TAIL, WO_TAIL, WO_SIDE = range(7)
 UP, DOWN, ACROSS, CORE = range(4)
 
 
@@ -71,9 +71,10 @@
     per_kv = heads_here // kv_here
     kv_cols = kv_here * HD
     kv_start = pl.multiple_of((head * heads_here // G) * HD, HD)
-    buffers = {WQ: wq, WKV: wkv, WO: wo, KV: kv, WQ_TAIL: wq, WO_TAIL: wo}
+    buffers = {WQ: wq, WKV: wkv, WO: wo, KV: kv, WQ_TAIL: wq, WO_TAIL: wo, WO_SIDE: wo}
     queries, outs = (WQ, WQ_TAIL), (WO, WO_TAIL)
     scale = 1.0 / math.sqrt(HD)
+    side = 16
 
     def slot_of(zz, yy, cc):
         return (zz * 2 + yy) * 2 + cc
@@ -83,7 +84,10 @@
         first, size = 0, each
         if item in queries + outs:
             cut = each // 2 // 16 * 16
-            first, size = (0, cut) if item in (WQ, WO) else (cut, each - cut)
+            end = each - side if item == WO_TAIL else each
+            first, size = (0, cut) if item in (WQ, WO) else (cut, end - cut)
+        if item == WO_SIDE:
+            first, size = each - side, side
         return buffers[item].at[pl.ds(pl.multiple_of(slot * each + first, 16), size)]
 
     def whole_rows(ref):
@@ -219,7 +223,7 @@
         send(WKV, me, route)
     own[0].wait()
     own[3].wait()
-    for item in queries + outs:
+    for item in queries + (WO_SIDE,) + outs:
         for route in (ACROSS, CORE):
             send(item, me, route)
 
@@ -286,13 +290,18 @@
             z_step(item, k, y, (ACROSS, CORE))
         z_step(KV, k, y, (ACROSS, CORE))
         if k == max(1, nz - 2):
-            for item in outs:
+            for item in (WO, WO_SIDE, WO_TAIL):
                 for route in (UP, DOWN):
                     send(item, me, route)
+            arrived(WO_SIDE, there)
+            for route in (UP, DOWN, CORE):
+                send(WO_SIDE, there, route)
     for k in range(1, nz):
         if k == nz - 1:
             for item in outs:
                 z_step(item, 1, y, (ACROSS, CORE))
+            for yy in (y, 1 - y):
+                z_step(WO_SIDE, 1, yy, (CORE,))
         for item in queries:
             across(item, k)
     for k in range(nz):
@@ -315,6 +324,8 @@
     if nz > 2:
         for item in outs:
             z_step(item, 2, y, (ACROSS, CORE))
+        for yy in (y, 1 - y):
+            z_step(WO_SIDE, 2, yy, (CORE,))
 
     keys = kv.shape[0]
     span = block_width(keys, 512)
@@ -369,6 +380,8 @@
                 z_step(WO, k, y, (ACROSS, CORE))
     for k in range(3, nz):
         z_step(WO_TAIL, k, y, (ACROSS, CORE))
+        for yy in (y, 1 - y):
+            z_step(WO_SIDE, k, yy, (CORE,))
 
     each = wo.shape[0] // blocks
     grouped = (4 * each) % HD == 0
@@ -410,7 +423,7 @@
             for item in outs:
                 arrived(item, slot)
                 send(item, slot, CORE)
-            for item in outs:
+            for item in outs + (WO_SIDE,):
                 for yy in range(2):
                     arrived(item, slot_of(zz, yy, 1 - c))
             produce(zz * 4 * each, chunk)
@@ -424,13 +437,14 @@
             for k in range(nz):
                 across(item, k)
             finish(item)
+        finish(WO_SIDE)
         part = 256
         lax.fori_loop(0, width // part, lambda n, carry: (produce(n * part, part), carry)[1], 0)
         for d in range(len(peers)):
             sum_copy(d, 0, 0).start()
 
-    for item in queries + outs + (WKV, KV):
-        drain(item, item == WKV)
+    for item in queries + outs + (WKV, KV, WO_SIDE):
+        drain(item, item in (WKV, WO_SIDE))
     for d in range(len(peers)):
         norm_copy(d).wait_send()
 
@@ -485,8 +499,8 @@
             pltpu.VMEM((group_rows, width), bf16),
             pltpu.VMEM((others, local_rows, width), bf16),
             pltpu.SemaphoreType.DMA((4,)),
-            pltpu.SemaphoreType.DMA((6, blocks, 4)),
-            pltpu.SemaphoreType.DMA((6, blocks)),
+            pltpu.SemaphoreType.DMA((7, blocks, 4)),
+            pltpu.SemaphoreType.DMA((7, blocks)),
             pltpu.SemaphoreType.DMA((others,)),
             pltpu.SemaphoreType.DMA((others,)),
             pltpu.SemaphoreType.DMA((others, blocks // 4)),

time: 161 us -> 164 us (1.019)
  Pallas kernels: 156 us -> 159 us
    pallas_call x1, Pallas kernels: 156 us -> 159 us  [on_device(): pl.pallas_call(functools.partial(kernel, (blocks, heads)), out_shape=jax....]
where the time goes in v4:
time: 164 us; the launch traced here: 163 us
  Pallas kernels  159 us (97%)
  local copies, waits for them, and re-layouts  3.7 us (2%)
    pallas_call x1, Pallas kernels, on_device(): pl.pallas_call(functools.partial(kernel, (blocks, heads)), out_shape=jax....  159 us

profile of v4, /device:TPU:0, one launch (start us, length us, event | category | flops | bytes accessed | tf_op | source)
XLA Modules:
  0.0 163.4 jit_solution(12119992636718890105)
XLA Ops:
  0.0 0.0 copy-start.1
  0.0 0.0 copy-start
  0.0 0.7 copy-done.1
  0.7 0.6 broadcast_in_dim.15.q_bias_ref
  1.3 0.0 copy-done
  1.3 0.6 broadcast_in_dim.14.gain_ref
  1.9 0.3 fusion
  2.2 0.7 pad_maximum_fusion
  3.0 158.6 %shard_map.91 = bf16[64,3584]{1,0:T(8,128)(2,1)} custom-call(bf16[64,3584]{1,0:T(8,128)(2,1)} %tokens_ref.1, f32[1,3584]{1,0:T(1,128)} %broadcast_in_dim.14.gain_ref, bf16[224,1536]{1,0:T(8,128)(2,1)} %w_query_ref.1, bf16[224,512]{1,0:T(8,128)(2,1)} %w_key_ref.1, bf16[224,512]{1,0:T(8,128)(2,1)} %w_value_ref.1, f32[1,1536]{1,0:T(1,128)} %broadcast_in_dim.15.q_bias_ref, ...), custom_call_target="tpu_custom_call" | custom-call | tf_op jit(solution)/shard_map/pallas_call | solution.py:485
  161.6 1.8 %copy.11 = bf16[64,3584]{1,0:T(8,128)(2,1)} copy(bf16[64,3584]{1,0:T(8,128)(2,1)} %shard_map.91) | data formatting | bytes 917504
  (2 shorter events, 0.0 us)
Async XLA Ops:
  0.0 0.7 copy-start.1
  0.0 1.3 copy-start
